TPU v7x, 128 devices: a whole 4x4x4 slice. The times are simulated.
128 devices in a mesh: head: 16 (over z, y), batch: 8 (over x, core).
Axes of the slice: x: 4, y: 4, z: 4, core: 2. Of those that a mesh axis runs over, the one named last changes fastest.
Arguments:
- incoming_hidden_stream: bfloat16 [1024, 4096], P('batch'), may hold values from -6 to 6
- reception_projection: bfloat16 [4096, 4096], P(None, 'head'), may hold values from -0.09375 to 0.09375
- address_projection: bfloat16 [4096, 4096], P(None, 'head'), may hold values from -0.09375 to 0.09375
- payload_projection: bfloat16 [4096, 4096], P(None, 'head'), may hold values from -0.09375 to 0.09375
- sigmoid_filter_matrix: bfloat16 [4096, 4096], P(None, 'head'), may hold values from -0.09375 to 0.09375
- forgetting_speed: float32 [1024, 4096], P('batch', 'head'), may hold values from 0.01 to 1.5
- adaptation_step_size: float32 [1024, 4096], P('batch', 'head'), may hold values from 0 to 1
- diagonal_boost: float32 [4096], P('head'), may hold values from -0.6 to 0.6
- subspace_standardize_scale: float32 [4096], P('head'), may hold values from 0.5 to 2
- recurrent_memory_matrix: float32 [128, 64, 64, 64], P('batch', 'head'), may hold values from -6 to 6
- emission_projection: bfloat16 [4096, 4096], P('head'), may hold values from -0.09375 to 0.09375
- closing_standardize_scale: float32 [4096], replicated, may hold values from 0.7 to 2
- lexicon_projection: bfloat16 [4096, 65536], P(None, ('head', 'batch')), may hold values from -32 to 32
- proposed_tokens_list: int32 [128, 8], P('batch'), may hold values from 0 to 65535
- threshold_milli_nats: int32 [128, 8], P('batch'), may hold values from -22000 to -10001
Outputs:
- new_state: float32 [128, 64, 64, 64], P('batch', 'head')
- margin: float32 [128, 8], P('batch')
- accept: float32 [128, 8], P('batch')
All inputs are finite; a program needn't handle non-finite values.
Results may differ from a plain program's by a relative error of at most 0.0017.
Values may be sent and summed in bfloat16 or wider, within the bound.
A program may use at most 128 MiB of HBM per device.

v0:
```python
import math

import jax
import jax.numpy as jnp
from jax import lax
from jax.sharding import Mesh
from jax.sharding import PartitionSpec as P

HEAD = ("head_0", "head_1")
HEAD_BATCH = ("head_0", "head_1", "batch")


def in_blocks(x, dim, size):
    before, after = (x.shape[:dim], x.shape[dim + 1 :])
    return jnp.moveaxis(x.reshape(*before, size, -1, *after), dim, 0)


def sent_and_summed(x, axis, dim):
    size = lax.axis_size(axis)
    parts = lax.all_to_all(in_blocks(x, dim, size), axis, 0, 0, tiled=True)
    return jnp.sum(parts, axis=0)


def by_axis(x, axes):
    for axis in axes:
        x = lax.psum(x, axis)
    return x


def joined_along(parts, dim):
    parts = jnp.moveaxis(parts, 0, dim)
    shape = parts.shape
    return parts.reshape(*shape[:dim], shape[dim] * shape[dim + 1], *shape[dim + 2 :])


def sent_to_all(x, axis):
    copies = jnp.broadcast_to(x, (lax.axis_size(axis), *x.shape))
    return lax.all_to_all(copies, axis, split_axis=0, concat_axis=0, tiled=True)


def gathered_copies(x, axis, dim):
    return joined_along(sent_to_all(x, axis), dim)


def gathered_once(x, axis):
    leaves = jax.tree.leaves(x)
    sequence = sorted(range(len(leaves)), key=lambda k: -leaves[k].size)
    width = (1, *leaves[sequence[0]].shape)[-1]
    lines = [
        jnp.pad(leaves[k].reshape(-1), (0, -leaves[k].size % width)).reshape(-1, width)
        for k in sequence
    ]
    both, at, found = (sent_to_all(jnp.concatenate(lines), axis), 0, {})
    for k, line in zip(sequence, lines):
        share = both[:, at : at + len(line)].reshape(len(both), -1)
        found[k] = share[:, : leaves[k].size].reshape(-1, *leaves[k].shape)
        at += len(line)
    numbers = iter(range(len(leaves)))
    return jax.tree.map(lambda _: found[next(numbers)], x)


def combined_pairwise(pieces, combine):
    while len(jax.tree.leaves(pieces)[0]) > 1:
        pieces = jax.vmap(combine)(
            *(jax.tree.map(lambda part: part[side::2], pieces) for side in (0, 1))
        )
    return jax.tree.map(lambda part: part[0], pieces)


def combined_all(x, axis, combine):
    pieces = gathered_once(x, axis)
    return combined_pairwise(pieces, combine)


def gathered_by_type(x, axis):
    leaves, found = (jax.tree.leaves(x), {})
    for initial, a in enumerate(leaves):
        if initial not in found:
            alike = [k for k, b in enumerate(leaves) if b.dtype == a.dtype]
            got = (
                gathered_once([leaves[k] for k in alike], axis)
                if len(alike) > 1
                else [sent_to_all(a, axis)]
            )
            for k, b in zip(alike, got):
                found[k] = b
    numbers = iter(range(len(leaves)))
    return jax.tree.map(lambda _: found[next(numbers)], x)


def merged(x, axis, combine):
    pieces = gathered_by_type(x, axis)
    return combined_pairwise(pieces, combine)


def advance(start, reception_vectors, address_vectors, payload_vectors, decay, rate):
    unit = (
        address_vectors
        * lax.rsqrt(jnp.mean(address_vectors * address_vectors, -1, keepdims=True) + 1e-06)
        / math.sqrt(address_vectors.shape[-1])
    )
    inputs = tuple(
        (
            jnp.moveaxis(item, 1, 0)
            for item in (reception_vectors, address_vectors, payload_vectors, decay, unit, rate)
        )
    )

    def step(current, pieces):
        recept_now, keys_now, values_now, decay_now, unit_now, rate_now = pieces
        recall = jnp.einsum("bhij,bhj->bhi", current, unit_now, precision=lax.Precision.HIGHEST)
        current = (
            current * decay_now[:, :, None, :]
            - recall[:, :, :, None] * (unit_now * rate_now)[:, :, None, :]
            + values_now[:, :, :, None] * keys_now[:, :, None, :]
        )
        output = jnp.einsum("bhij,bhj->bhi", current, recept_now, precision=lax.Precision.HIGHEST)
        return (current, output)

    final, outputs = lax.scan(step, start, inputs)
    return (final, jnp.moveaxis(outputs, 0, 1))


def combine_stats(first, second):
    top = jnp.maximum(first[0], second[0])
    summed = first[1] * jnp.exp(first[0] - top) + second[1] * jnp.exp(second[0] - top)
    return (top, summed, first[2] + second[2])


def local_stats(logits, ids_flat, offset):
    peak = jnp.max(logits, -1)
    total = jnp.sum(jnp.exp(logits - peak[:, None]), -1)
    column = lax.broadcasted_iota(jnp.int32, logits.shape, 1)
    target = jnp.sum(jnp.where(column == (ids_flat - offset)[:, None], logits, 0.0), -1)
    return (peak, total, target)


def shards(
    incoming_hidden_stream,
    reception_projection,
    address_projection,
    payload_projection,
    sigmoid_filter_matrix,
    forgetting_speed,
    adaptation_step_size,
    diagonal_boost,
    subspace_standardize_scale,
    recurrent_memory_matrix,
    emission_projection,
    closing_standardize_scale,
    lexicon_projection,
    proposed_tokens_list,
    threshold_milli_nats,
):
    seq_dev, draft_len = proposed_tokens_list.shape
    lanes_on_shard, subspace_size = (
        recurrent_memory_matrix.shape[1],
        recurrent_memory_matrix.shape[2],
    )
    tok_dev = seq_dev * draft_len
    width = incoming_hidden_stream.shape[1]
    shape4 = (seq_dev, draft_len, lanes_on_shard, subspace_size)
    reception_vectors = jnp.dot(
        incoming_hidden_stream, reception_projection, preferred_element_type=jnp.float32
    ).reshape(shape4)
    address_vectors = jnp.dot(
        incoming_hidden_stream, address_projection, preferred_element_type=jnp.float32
    ).reshape(shape4)
    payload_vectors = jnp.dot(
        incoming_hidden_stream, payload_projection, preferred_element_type=jnp.float32
    ).reshape(shape4)
    gate = jnp.dot(
        incoming_hidden_stream, sigmoid_filter_matrix, preferred_element_type=jnp.float32
    )
    decay = jnp.exp(-forgetting_speed).reshape(shape4)
    rate = adaptation_step_size.reshape(shape4)
    new_state, wkv = advance(
        recurrent_memory_matrix, reception_vectors, address_vectors, payload_vectors, decay, rate
    )
    center = wkv - jnp.mean(wkv, -1, keepdims=True)
    interpolated_embedding = (
        center
        * lax.rsqrt(jnp.mean(center * center, -1, keepdims=True) + 1e-05)
        * subspace_standardize_scale.reshape(lanes_on_shard, subspace_size)
    )
    interpolated_embedding = (
        interpolated_embedding
        + jnp.sum(
            reception_vectors
            * address_vectors
            * diagonal_boost.reshape(lanes_on_shard, subspace_size),
            -1,
            keepdims=True,
        )
        * payload_vectors
    )
    gated = (
        interpolated_embedding.reshape(tok_dev, lanes_on_shard * subspace_size)
        * jax.nn.sigmoid(gate)
    ).astype(jnp.bfloat16)
    partial_out = jnp.dot(gated, emission_projection, preferred_element_type=jnp.float32)
    share = sent_and_summed(partial_out, HEAD, 1)
    cols = share.shape[1]
    begin = lax.axis_index(HEAD) * cols
    residual = (
        lax.dynamic_slice_in_dim(incoming_hidden_stream, begin, cols, 1).astype(jnp.float32) + share
    )
    moment_one, moment_two = (
        by_axis(jnp.sum(residual, -1), HEAD),
        by_axis(jnp.sum(residual * residual, -1), HEAD),
    )
    mean_row = moment_one / width
    variance = moment_two / width - mean_row * mean_row
    gain_part = lax.dynamic_slice_in_dim(closing_standardize_scale, begin, cols, 0)
    normed_part = (
        (residual - mean_row[:, None]) * lax.rsqrt(variance + 1e-05)[:, None] * gain_part
    ).astype(jnp.bfloat16)
    normed = gathered_copies(normed_part, HEAD, 1)
    every, every_ids = (
        lax.all_gather(normed, "batch", axis=0, tiled=True),
        lax.all_gather(proposed_tokens_list, "batch", axis=0, tiled=True),
    )
    logits = jnp.dot(every, lexicon_projection, preferred_element_type=jnp.float32)
    vcols = lexicon_projection.shape[1]
    offset = (lax.axis_index(HEAD) * lax.axis_size("batch") + lax.axis_index("batch")) * vcols
    peak, total, target = local_stats(logits, every_ids.reshape(-1), offset)
    peak, total, target = combined_all((peak, total, target), "batch", combine_stats)
    row_begin = lax.axis_index("batch") * tok_dev
    peak = lax.dynamic_slice_in_dim(peak, row_begin, tok_dev, 0)
    total = lax.dynamic_slice_in_dim(total, row_begin, tok_dev, 0)
    target = lax.dynamic_slice_in_dim(target, row_begin, tok_dev, 0)
    top, summed, target = merged((peak, total, target), HEAD, combine_stats)
    logprob = target - (top + jnp.log(summed))
    margin = logprob.reshape(seq_dev, draft_len) - threshold_milli_nats.astype(jnp.float32) / 1000.0
    accept = jnp.cumprod(jax.nn.sigmoid(margin * 0.5), axis=1)
    return (new_state, margin, accept)


def solution(mesh):
    split = Mesh(mesh.devices.reshape(4, 4, mesh.shape["batch"]), ("head_0", "head_1", "batch"))
    return jax.shard_map(
        shards,
        mesh=split,
        in_specs=(
            P("batch", None),
            P(None, HEAD),
            P(None, HEAD),
            P(None, HEAD),
            P(None, HEAD),
            P("batch", HEAD),
            P("batch", HEAD),
            P(HEAD),
            P(HEAD),
            P("batch", HEAD, None, None),
            P(HEAD, None),
            P(),
            P(None, HEAD_BATCH),
            P("batch", None),
            P("batch", None),
        ),
        out_specs=(P("batch", HEAD, None, None), P("batch", None), P("batch", None)),
        check_vma=False,
    )
```

profile of v0, /device:TPU:0, one launch (start us, length us, event | category | flops | bytes accessed | tf_op | source)
XLA Modules:
  0.0 318.9 jit_solution(11417522193714851282)
XLA Ops:
  7.2 3.3 %copy.146 = f32[16,4,64,64]{3,2,1,0:T(8,128)} copy(f32[16,4,64,64]{3,2,1,0:T(8,128)} %param.26) | data formatting | bytes 2097152
  12.3 2.0 fusion.26
  15.2 2.0 fusion.28
  18.2 2.0 multiply_reduce_fusion
  20.5 1.9 copy_bitcast_fusion.2
  22.3 1.8 reshape.126
  24.1 2.0 fusion.27
  27.0 2.0 copy_bitcast_fusion
  29.0 105.4 %while.12 = (s32[]{:T(128)}, f32[16,4,64,64]{3,2,1,0:T(8,128)}, f32[8,16,4,64]{3,2,1,0:T(4,128)S(1)}, f32[8,16,4,64]{3,2,0,1:T(4,128)}, f32[8,16,4,64]{3,2,1,0:T...) while((s32[]{:T(128)}, f32[16,4,64,64]{3,2,1,0:T(8,128)}, ...), condition=%wide.region_2.3_spmd, body=%wide.region_1.2_spmd.sunk | while | flops 7606274 | bytes 13009081 | solution.py:120
  31.5 4.9 %fusion.54 = f32[16,4,1,64]{3,2,1,0:T(1,128)S(1)} fusion(f32[16,4,64,1]{2,3,1,0:T(1,128)S(1)} %bitcast.118, f32[16,4,64,64]{3,2,1,0:T(8,128)} %get-tuple-element.245), kind=kOutput, calls=%fused_computation.79.clone.1 | convolution fusion | flops 3145728 | bytes 1081344 | tf_op jit(solution)/shard_map/while/body/eval_jaxpr/bhij,bhj->bhi/dot_general | solution.py:111
  37.2 1.5 multiply_add_fusion.8
  38.8 3.3 %fusion.55 = f32[16,4,1,64]{3,2,1,0:T(1,128)S(1)} fusion(f32[16,4,64,64]{3,2,1,0:T(8,128)S(1)} %multiply_add_fusion.8, f32[16,4,64,1]{2,3,1,0:T(1,128)S(1)} %bitcast.117), kind=kOutput, calls=%fused_computation.80.clone.1 | convolution fusion | flops 3145728 | bytes 1081344 | tf_op jit(solution)/shard_map/while/body/eval_jaxpr/bhij,bhj->bhi/dot_general | solution.py:117
  44.7 4.9 %fusion.54 = f32[16,4,1,64]{3,2,1,0:T(1,128)S(1)} fusion(f32[16,4,64,1]{2,3,1,0:T(1,128)S(1)} %bitcast.118, f32[16,4,64,64]{3,2,1,0:T(8,128)} %get-tuple-element.245), kind=kOutput, calls=%fused_computation.79.clone.1 | convolution fusion | flops 3145728 | bytes 1081344 | tf_op jit(solution)/shard_map/while/body/eval_jaxpr/bhij,bhj->bhi/dot_general | solution.py:111
  50.4 1.5 multiply_add_fusion.8
  52.0 3.3 %fusion.55 = f32[16,4,1,64]{3,2,1,0:T(1,128)S(1)} fusion(f32[16,4,64,64]{3,2,1,0:T(8,128)S(1)} %multiply_add_fusion.8, f32[16,4,64,1]{2,3,1,0:T(1,128)S(1)} %bitcast.117), kind=kOutput, calls=%fused_computation.80.clone.1 | convolution fusion | flops 3145728 | bytes 1081344 | tf_op jit(solution)/shard_map/while/body/eval_jaxpr/bhij,bhj->bhi/dot_general | solution.py:117
  57.9 4.9 %fusion.54 = f32[16,4,1,64]{3,2,1,0:T(1,128)S(1)} fusion(f32[16,4,64,1]{2,3,1,0:T(1,128)S(1)} %bitcast.118, f32[16,4,64,64]{3,2,1,0:T(8,128)} %get-tuple-element.245), kind=kOutput, calls=%fused_computation.79.clone.1 | convolution fusion | flops 3145728 | bytes 1081344 | tf_op jit(solution)/shard_map/while/body/eval_jaxpr/bhij,bhj->bhi/dot_general | solution.py:111
  63.6 1.5 multiply_add_fusion.8
  65.1 3.3 %fusion.55 = f32[16,4,1,64]{3,2,1,0:T(1,128)S(1)} fusion(f32[16,4,64,64]{3,2,1,0:T(8,128)S(1)} %multiply_add_fusion.8, f32[16,4,64,1]{2,3,1,0:T(1,128)S(1)} %bitcast.117), kind=kOutput, calls=%fused_computation.80.clone.1 | convolution fusion | flops 3145728 | bytes 1081344 | tf_op jit(solution)/shard_map/while/body/eval_jaxpr/bhij,bhj->bhi/dot_general | solution.py:117
  71.0 4.9 %fusion.54 = f32[16,4,1,64]{3,2,1,0:T(1,128)S(1)} fusion(f32[16,4,64,1]{2,3,1,0:T(1,128)S(1)} %bitcast.118, f32[16,4,64,64]{3,2,1,0:T(8,128)} %get-tuple-element.245), kind=kOutput, calls=%fused_computation.79.clone.1 | convolution fusion | flops 3145728 | bytes 1081344 | tf_op jit(solution)/shard_map/while/body/eval_jaxpr/bhij,bhj->bhi/dot_general | solution.py:111
  76.8 1.5 multiply_add_fusion.8
  78.3 3.3 %fusion.55 = f32[16,4,1,64]{3,2,1,0:T(1,128)S(1)} fusion(f32[16,4,64,64]{3,2,1,0:T(8,128)S(1)} %multiply_add_fusion.8, f32[16,4,64,1]{2,3,1,0:T(1,128)S(1)} %bitcast.117), kind=kOutput, calls=%fused_computation.80.clone.1 | convolution fusion | flops 3145728 | bytes 1081344 | tf_op jit(solution)/shard_map/while/body/eval_jaxpr/bhij,bhj->bhi/dot_general | solution.py:117
  84.2 4.9 %fusion.54 = f32[16,4,1,64]{3,2,1,0:T(1,128)S(1)} fusion(f32[16,4,64,1]{2,3,1,0:T(1,128)S(1)} %bitcast.118, f32[16,4,64,64]{3,2,1,0:T(8,128)} %get-tuple-element.245), kind=kOutput, calls=%fused_computation.79.clone.1 | convolution fusion | flops 3145728 | bytes 1081344 | tf_op jit(solution)/shard_map/while/body/eval_jaxpr/bhij,bhj->bhi/dot_general | solution.py:111
  89.9 1.5 multiply_add_fusion.8
  91.5 3.3 %fusion.55 = f32[16,4,1,64]{3,2,1,0:T(1,128)S(1)} fusion(f32[16,4,64,64]{3,2,1,0:T(8,128)S(1)} %multiply_add_fusion.8, f32[16,4,64,1]{2,3,1,0:T(1,128)S(1)} %bitcast.117), kind=kOutput, calls=%fused_computation.80.clone.1 | convolution fusion | flops 3145728 | bytes 1081344 | tf_op jit(solution)/shard_map/while/body/eval_jaxpr/bhij,bhj->bhi/dot_general | solution.py:117
  97.4 4.9 %fusion.54 = f32[16,4,1,64]{3,2,1,0:T(1,128)S(1)} fusion(f32[16,4,64,1]{2,3,1,0:T(1,128)S(1)} %bitcast.118, f32[16,4,64,64]{3,2,1,0:T(8,128)} %get-tuple-element.245), kind=kOutput, calls=%fused_computation.79.clone.1 | convolution fusion | flops 3145728 | bytes 1081344 | tf_op jit(solution)/shard_map/while/body/eval_jaxpr/bhij,bhj->bhi/dot_general | solution.py:111
  103.1 1.5 multiply_add_fusion.8
  104.7 3.3 %fusion.55 = f32[16,4,1,64]{3,2,1,0:T(1,128)S(1)} fusion(f32[16,4,64,64]{3,2,1,0:T(8,128)S(1)} %multiply_add_fusion.8, f32[16,4,64,1]{2,3,1,0:T(1,128)S(1)} %bitcast.117), kind=kOutput, calls=%fused_computation.80.clone.1 | convolution fusion | flops 3145728 | bytes 1081344 | tf_op jit(solution)/shard_map/while/body/eval_jaxpr/bhij,bhj->bhi/dot_general | solution.py:117
  110.6 4.9 %fusion.54 = f32[16,4,1,64]{3,2,1,0:T(1,128)S(1)} fusion(f32[16,4,64,1]{2,3,1,0:T(1,128)S(1)} %bitcast.118, f32[16,4,64,64]{3,2,1,0:T(8,128)} %get-tuple-element.245), kind=kOutput, calls=%fused_computation.79.clone.1 | convolution fusion | flops 3145728 | bytes 1081344 | tf_op jit(solution)/shard_map/while/body/eval_jaxpr/bhij,bhj->bhi/dot_general | solution.py:111
  116.3 1.5 multiply_add_fusion.8
  117.9 3.3 %fusion.55 = f32[16,4,1,64]{3,2,1,0:T(1,128)S(1)} fusion(f32[16,4,64,64]{3,2,1,0:T(8,128)S(1)} %multiply_add_fusion.8, f32[16,4,64,1]{2,3,1,0:T(1,128)S(1)} %bitcast.117), kind=kOutput, calls=%fused_computation.80.clone.1 | convolution fusion | flops 3145728 | bytes 1081344 | tf_op jit(solution)/shard_map/while/body/eval_jaxpr/bhij,bhj->bhi/dot_general | solution.py:117
  123.8 4.9 %fusion.54 = f32[16,4,1,64]{3,2,1,0:T(1,128)S(1)} fusion(f32[16,4,64,1]{2,3,1,0:T(1,128)S(1)} %bitcast.118, f32[16,4,64,64]{3,2,1,0:T(8,128)} %get-tuple-element.245), kind=kOutput, calls=%fused_computation.79.clone.1 | convolution fusion | flops 3145728 | bytes 1081344 | tf_op jit(solution)/shard_map/while/body/eval_jaxpr/bhij,bhj->bhi/dot_general | solution.py:111
  129.5 1.5 multiply_add_fusion.8
  131.1 3.3 %fusion.55 = f32[16,4,1,64]{3,2,1,0:T(1,128)S(1)} fusion(f32[16,4,64,64]{3,2,1,0:T(8,128)S(1)} %multiply_add_fusion.8, f32[16,4,64,1]{2,3,1,0:T(1,128)S(1)} %bitcast.117), kind=kOutput, calls=%fused_computation.80.clone.1 | convolution fusion | flops 3145728 | bytes 1081344 | tf_op jit(solution)/shard_map/while/body/eval_jaxpr/bhij,bhj->bhi/dot_general | solution.py:117
  139.9 4.2 %fusion.5 = f32[128,4096]{1,0:T(8,128)} fusion(bf16[256,4096]{1,0:T(8,128)(2,1)S(1)} %copy-done, f32[128,256]{1,0:T(8,128)S(1)} %reshape.129, bf16[128,4096]{1,0:T(8,128)(2,1)S(1)} %copy-done.3, bf16[4096,256]{1,0:T(8,128)(2,1)} %param.21), kind=kOutput, calls=%fused_computation.18 | convolution fusion | flops 537034752 | bytes 7471104 | tf_op jit(solution)/shard_map/dot_general | solution.py:201
  144.2 3.2 copy.131
  147.3 8.2 %all-to-all-start = ((f32[16,128,256]{2,1,0:T(8,128)}), f32[16,128,256]{2,1,0:T(8,128)}, u32[]{:S(2)}, u32[]{:S(2)}) async-start(f32[16,128,256]{2,1,0:T(8,128)} %bitcast.113), calls=%async_computation | async-start | bytes 4194304 | tf_op jit(solution)/shard_map/all_to_all | solution.py:20
  156.4 31.0 %all-to-all-done = f32[16,128,256]{2,1,0:T(8,128)} async-done(((f32[16,128,256]{2,1,0:T(8,128)}), f32[16,128,256]{2,1,0:T(8,128)}, u32[]{:S(2)}, u32[]{:S(2)}) %all-to-all-start) | async-done | bytes 2097184 | tf_op jit(solution)/shard_map/all_to_all | solution.py:20
  187.4 1.7 reduce_sum.85
  189.2 9.5 %all-reduce.1 = (f32[128]{0:T(128)S(1)}, f32[128]{0:T(128)S(1)}) all-reduce(f32[128]{0:T(128)S(1)} %get-tuple-element.107, f32[128]{0:T(128)S(1)} %get-tuple-element.106), channel_id=1, replica_groups=mesh['head_0'=4,'head_1'=4,'batch'=8] {'head_0'}, use_global_device_ids=true, to_apply=%region_11.12 | all-reduce | flops 256 | bytes 2048 | tf_op jit(solution)/shard_map/psum | solution.py:26
  198.7 7.7 %all-reduce = (f32[128]{0:T(128)S(1)}, f32[128]{0:T(128)S(1)}) all-reduce(f32[128]{0:T(128)S(1)} %get-tuple-element.130, f32[128]{0:T(128)S(1)} %get-tuple-element.131), channel_id=1, replica_groups=mesh['head_0'=4,'head_1'=4,'batch'=8] {'head_1'}, use_global_device_ids=true, to_apply=%region_12.13 | all-reduce | flops 256 | bytes 2048 | tf_op jit(solution)/shard_map/psum | solution.py:26
  206.9 16.6 %all_to_all.20 = bf16[16,128,256]{1,2,0:T(8,128)(2,1)} all-to-all(bf16[16,128,256]{1,2,0:T(8,128)(2,1)S(1)} %broadcast_in_dim.21), channel_id=1, replica_groups=mesh['head_0'=4,'head_1'=4,'batch'=8] {'head_0','head_1'}, dimensions={0} | all-to-all | bytes 2097152 | tf_op jit(solution)/shard_map/all_to_all | solution.py:38
  223.5 13.3 %all-gather = s32[8,16,8]{1,2,0:T(8,128)S(1)} all-gather(s32[1,16,8]{1,2,0:T(8,128)S(1)} %bitcast.136), channel_id=1, replica_groups=mesh['head_0'=4,'head_1'=4,'batch'=8] {'batch'}, dimensions={0}, use_global_device_ids=true | all-gather | bytes 4608 | tf_op jit(solution)/shard_map/all_gather | solution.py:221
  237.0 37.6 %all-gather.3.cloned.1.call-done = bf16[1024,4096]{0,1:T(8,128)(2,1)} async-done(((bf16[128,4096]{0,1:T(8,128)(2,1)}), bf16[1024,4096]{0,1:T(8,128)(2,1)}) %all-gather.3.cloned.1.call-update) | async-done | bytes 8388624 | tf_op jit(solution)/shard_map/all_gather | solution.py:220
  274.6 8.3 %fusion.23 = (f32[1024]{0:T(1024)S(1)}, f32[1024,512]{0,1:T(8,128)S(1)}) fusion(bf16[1024,4096]{0,1:T(8,128)(2,1)} %all-gather.3.cloned.1.call-done, bf16[4096,512]{1,0:T(8,128)(2,1)} %param.29), kind=kOutput, calls=%fused_computation.78 | convolution fusion | flops 4295490560 | bytes 14684160 | tf_op jit(solution)/shard_map/dot_general | solution.py:223
  284.1 4.0 %all-to-all-start.2 = ((f32[8,3,1024]{2,1,0:T(4,128)}), f32[8,3,1024]{2,1,0:T(4,128)S(1)}, u32[]{:S(2)}, u32[]{:S(2)}) async-start(f32[8,3,1024]{2,1,0:T(4,128)} %broadcast_in_dim.23), calls=%async_computation.2 | async-start | bytes 262144 | tf_op jit(solution)/shard_map/all_to_all | solution.py:38
  288.1 6.1 %all-to-all-done.2 = f32[8,3,1024]{2,1,0:T(4,128)S(1)} async-done(((f32[8,3,1024]{2,1,0:T(4,128)}), f32[8,3,1024]{2,1,0:T(4,128)S(1)}, u32[]{:S(2)}, u32[]{:S(2)}) %all-to-all-start.2) | async-done | bytes 98336 | tf_op jit(solution)/shard_map/all_to_all | solution.py:38
  295.4 6.9 %all-to-all-start.3 = ((f32[16,3,128]{2,1,0:T(4,128)}), f32[16,3,128]{2,1,0:T(4,128)S(1)}, u32[]{:S(2)}, u32[]{:S(2)}) async-start(f32[16,3,128]{2,1,0:T(4,128)} %broadcast_in_dim.25), calls=%async_computation.3 | async-start | bytes 65536 | tf_op jit(solution)/shard_map/all_to_all | solution.py:38
  302.5 7.5 %all-to-all-done.3 = f32[16,3,128]{2,1,0:T(4,128)S(1)} async-done(((f32[16,3,128]{2,1,0:T(4,128)}), f32[16,3,128]{2,1,0:T(4,128)S(1)}, u32[]{:S(2)}, u32[]{:S(2)}) %all-to-all-start.3) | async-done | bytes 24608 | tf_op jit(solution)/shard_map/all_to_all | solution.py:38
  (182 shorter events, 42.6 us)
Async XLA Ops:
  7.2 132.8 %copy-start = (bf16[256,4096]{1,0:T(8,128)(2,1)S(1)}, bf16[256,4096]{1,0:T(8,128)(2,1)}, u32[]{:S(2)}) copy-start(bf16[256,4096]{1,0:T(8,128)(2,1)} %param.27) | copy-start | bytes 6291460
  7.2 5.1 %copy-start.3 = (bf16[128,4096]{1,0:T(8,128)(2,1)S(1)}, bf16[128,4096]{1,0:T(8,128)(2,1)}, u32[]{:S(2)}) copy-start(bf16[128,4096]{1,0:T(8,128)(2,1)} %param.17) | copy-start | bytes 3145732
  14.3 3.7 %copy-start.7 = (f32[256]{0:T(256)S(1)}, f32[256]{0:T(256)}, u32[]{:S(2)}) copy-start(f32[256]{0:T(256)} %param.24) | copy-start | bytes 3076
  29.0 105.5 %copy-start.4 = (f32[16,8,4]{2,1,0:T(8,128)S(1)}, f32[16,8,4]{2,1,0:T(8,128)}, u32[]{:S(2)}) copy-start(f32[16,8,4]{2,1,0:T(8,128)} %get-tuple-element.108) | copy-start | bytes 6148
  29.0 106.1 %copy-start.8 = (f32[256]{0:T(256)S(1)}, f32[256]{0:T(256)}, u32[]{:S(2)}) copy-start(f32[256]{0:T(256)} %param.25) | copy-start | bytes 3076
  29.0 8.2 %copy-start.1 = (f32[16,4,64,64]{3,2,1,0:T(8,128)S(1)}, f32[16,4,64,64]{3,2,1,0:T(8,128)}, u32[]{:S(2)}) copy-start(f32[16,4,64,64]{3,2,1,0:T(8,128)} %get-tuple-element.245) | copy-start | bytes 3145732 | tf_op jit(solution)/shard_map/while
  38.8 3.4 %copy-start.2 = (f32[16,4,64,64]{3,2,1,0:T(8,128)}, f32[16,4,64,64]{3,2,1,0:T(8,128)S(1)}, u32[]{:S(2)}) copy-start(f32[16,4,64,64]{3,2,1,0:T(8,128)S(1)} %multiply_add_fusion.8) | copy-start | bytes 3145732 | tf_op jit(solution)/shard_map/while
  42.2 8.2 %copy-start.1 = (f32[16,4,64,64]{3,2,1,0:T(8,128)S(1)}, f32[16,4,64,64]{3,2,1,0:T(8,128)}, u32[]{:S(2)}) copy-start(f32[16,4,64,64]{3,2,1,0:T(8,128)} %get-tuple-element.245) | copy-start | bytes 3145732 | tf_op jit(solution)/shard_map/while
  51.9 3.4 %copy-start.2 = (f32[16,4,64,64]{3,2,1,0:T(8,128)}, f32[16,4,64,64]{3,2,1,0:T(8,128)S(1)}, u32[]{:S(2)}) copy-start(f32[16,4,64,64]{3,2,1,0:T(8,128)S(1)} %multiply_add_fusion.8) | copy-start | bytes 3145732 | tf_op jit(solution)/shard_map/while
  55.3 8.2 %copy-start.1 = (f32[16,4,64,64]{3,2,1,0:T(8,128)S(1)}, f32[16,4,64,64]{3,2,1,0:T(8,128)}, u32[]{:S(2)}) copy-start(f32[16,4,64,64]{3,2,1,0:T(8,128)} %get-tuple-element.245) | copy-start | bytes 3145732 | tf_op jit(solution)/shard_map/while
  65.1 3.4 %copy-start.2 = (f32[16,4,64,64]{3,2,1,0:T(8,128)}, f32[16,4,64,64]{3,2,1,0:T(8,128)S(1)}, u32[]{:S(2)}) copy-start(f32[16,4,64,64]{3,2,1,0:T(8,128)S(1)} %multiply_add_fusion.8) | copy-start | bytes 3145732 | tf_op jit(solution)/shard_map/while
  68.5 8.2 %copy-start.1 = (f32[16,4,64,64]{3,2,1,0:T(8,128)S(1)}, f32[16,4,64,64]{3,2,1,0:T(8,128)}, u32[]{:S(2)}) copy-start(f32[16,4,64,64]{3,2,1,0:T(8,128)} %get-tuple-element.245) | copy-start | bytes 3145732 | tf_op jit(solution)/shard_map/while
  78.3 3.4 %copy-start.2 = (f32[16,4,64,64]{3,2,1,0:T(8,128)}, f32[16,4,64,64]{3,2,1,0:T(8,128)S(1)}, u32[]{:S(2)}) copy-start(f32[16,4,64,64]{3,2,1,0:T(8,128)S(1)} %multiply_add_fusion.8) | copy-start | bytes 3145732 | tf_op jit(solution)/shard_map/while
  81.7 8.2 %copy-start.1 = (f32[16,4,64,64]{3,2,1,0:T(8,128)S(1)}, f32[16,4,64,64]{3,2,1,0:T(8,128)}, u32[]{:S(2)}) copy-start(f32[16,4,64,64]{3,2,1,0:T(8,128)} %get-tuple-element.245) | copy-start | bytes 3145732 | tf_op jit(solution)/shard_map/while
  91.5 3.4 %copy-start.2 = (f32[16,4,64,64]{3,2,1,0:T(8,128)}, f32[16,4,64,64]{3,2,1,0:T(8,128)S(1)}, u32[]{:S(2)}) copy-start(f32[16,4,64,64]{3,2,1,0:T(8,128)S(1)} %multiply_add_fusion.8) | copy-start | bytes 3145732 | tf_op jit(solution)/shard_map/while
  94.9 8.2 %copy-start.1 = (f32[16,4,64,64]{3,2,1,0:T(8,128)S(1)}, f32[16,4,64,64]{3,2,1,0:T(8,128)}, u32[]{:S(2)}) copy-start(f32[16,4,64,64]{3,2,1,0:T(8,128)} %get-tuple-element.245) | copy-start | bytes 3145732 | tf_op jit(solution)/shard_map/while
  104.7 3.4 %copy-start.2 = (f32[16,4,64,64]{3,2,1,0:T(8,128)}, f32[16,4,64,64]{3,2,1,0:T(8,128)S(1)}, u32[]{:S(2)}) copy-start(f32[16,4,64,64]{3,2,1,0:T(8,128)S(1)} %multiply_add_fusion.8) | copy-start | bytes 3145732 | tf_op jit(solution)/shard_map/while
  108.1 8.2 %copy-start.1 = (f32[16,4,64,64]{3,2,1,0:T(8,128)S(1)}, f32[16,4,64,64]{3,2,1,0:T(8,128)}, u32[]{:S(2)}) copy-start(f32[16,4,64,64]{3,2,1,0:T(8,128)} %get-tuple-element.245) | copy-start | bytes 3145732 | tf_op jit(solution)/shard_map/while
  117.9 3.4 %copy-start.2 = (f32[16,4,64,64]{3,2,1,0:T(8,128)}, f32[16,4,64,64]{3,2,1,0:T(8,128)S(1)}, u32[]{:S(2)}) copy-start(f32[16,4,64,64]{3,2,1,0:T(8,128)S(1)} %multiply_add_fusion.8) | copy-start | bytes 3145732 | tf_op jit(solution)/shard_map/while
  121.3 8.2 %copy-start.1 = (f32[16,4,64,64]{3,2,1,0:T(8,128)S(1)}, f32[16,4,64,64]{3,2,1,0:T(8,128)}, u32[]{:S(2)}) copy-start(f32[16,4,64,64]{3,2,1,0:T(8,128)} %get-tuple-element.245) | copy-start | bytes 3145732 | tf_op jit(solution)/shard_map/while
  131.0 3.4 %copy-start.2 = (f32[16,4,64,64]{3,2,1,0:T(8,128)}, f32[16,4,64,64]{3,2,1,0:T(8,128)S(1)}, u32[]{:S(2)}) copy-start(f32[16,4,64,64]{3,2,1,0:T(8,128)S(1)} %multiply_add_fusion.8) | copy-start | bytes 3145732 | tf_op jit(solution)/shard_map/while
  147.3 40.1 %all-to-all-start = ((f32[16,128,256]{2,1,0:T(8,128)}), f32[16,128,256]{2,1,0:T(8,128)}, u32[]{:S(2)}, u32[]{:S(2)}) async-start(f32[16,128,256]{2,1,0:T(8,128)} %bitcast.113), calls=%async_computation | async-start | bytes 4194304 | tf_op jit(solution)/shard_map/all_to_all | solution.py:20
  155.5 119.1 %all-gather.3.cloned.1.call-start = ((), (), s32[]{:S(2)}) async-start(), calls=%async_computation.4 | async-start | bytes 9437184 | tf_op jit(solution)/shard_map/all_gather | solution.py:220
  206.7 16.9 %copy-start.5 = (s32[16,8]{0,1:T(8,128)S(1)}, s32[16,8]{0,1:T(8,128)}, u32[]{:S(2)}) copy-start(s32[16,8]{0,1:T(8,128)} %param.30) | copy-start | bytes 1540
  282.9 19.5 %copy-start.6 = (s32[16,8]{0,1:T(8,128)S(1)}, s32[16,8]{0,1:T(8,128)}, u32[]{:S(2)}) copy-start(s32[16,8]{0,1:T(8,128)} %param.31) | copy-start | bytes 1540
  284.1 10.1 %all-to-all-start.2 = ((f32[8,3,1024]{2,1,0:T(4,128)}), f32[8,3,1024]{2,1,0:T(4,128)S(1)}, u32[]{:S(2)}, u32[]{:S(2)}) async-start(f32[8,3,1024]{2,1,0:T(4,128)} %broadcast_in_dim.23), calls=%async_computation.2 | async-start | bytes 262144 | tf_op jit(solution)/shard_map/all_to_all | solution.py:38
  295.4 14.6 %all-to-all-start.3 = ((f32[16,3,128]{2,1,0:T(4,128)}), f32[16,3,128]{2,1,0:T(4,128)S(1)}, u32[]{:S(2)}, u32[]{:S(2)}) async-start(f32[16,3,128]{2,1,0:T(4,128)} %broadcast_in_dim.25), calls=%async_computation.3 | async-start | bytes 65536 | tf_op jit(solution)/shard_map/all_to_all | solution.py:38
Sparse Core Ops, SparseCore 0:
  223.6 50.9 all-gather.2
where the time goes:
time: 321 us; the launch traced here: 319 us
  matrix products  84.9 us (26%)
  waiting for transfers between devices  82.3 us (26%)
  blocking collectives  47.1 us (15%)
  local copies, waits for them, and re-layouts  41.7 us (13%)
  other arithmetic  29.1 us (9%)
  starting transfers between devices  19.2 us (6%)
  between operations  14.4 us (4%)
    dot_general x8, matrix products, step(): jnp.einsum('bhij,bhj->bhi', current, unit_now, precision=lax.Precision.HI...  39.5 us
    all_gather x1, waiting for transfers between devices, shards(): lax.all_gather(normed, 'batch', axis=0, tiled=True)  37.6 us
    all_to_all x1, waiting for transfers between devices, sent_and_summed(): parts = lax.all_to_all(in_blocks(x, dim, size), axis, 0, 0, tiled=True)  31 us
    dot_general x8, matrix products, step(): jnp.einsum('bhij,bhj->bhi', current, recept_now, precision=lax.Precision....  26.8 us
    psum x2, blocking collectives, by_axis(): x = lax.psum(x, axis)  17.2 us
    all_to_all x1, blocking collectives, sent_to_all(): return lax.all_to_all(copies, axis, split_axis=0, concat_axis=0, tiled=True)  16.6 us
    all_to_all x2, waiting for transfers between devices, sent_to_all(): return lax.all_to_all(copies, axis, split_axis=0, concat_axis=0, tiled=True)  13.6 us
    all_gather x1, blocking collectives, shards(): lax.all_gather(proposed_tokens_list, 'batch', axis=0, tiled=True)  13.3 us
  transfers between devices with their start and end apart: 4, of which 4 were waited for; matrix products, arithmetic and copies ran while one was open for 0% of the time, Pallas kernels for 0%

commit v1 on v0

--- a/solution.py
+++ b/solution.py
@@ -3,6 +3,8 @@
 import jax
 import jax.numpy as jnp
 from jax import lax
+from jax.experimental import pallas as pl
+from jax.experimental.pallas import tpu as pltpu
 from jax.sharding import Mesh
 from jax.sharding import PartitionSpec as P
 
@@ -93,32 +95,120 @@
     return combined_pairwise(pieces, combine)
 
 
-def advance(start, reception_vectors, address_vectors, payload_vectors, decay, rate):
-    unit = (
-        address_vectors
-        * lax.rsqrt(jnp.mean(address_vectors * address_vectors, -1, keepdims=True) + 1e-06)
-        / math.sqrt(address_vectors.shape[-1])
-    )
-    inputs = tuple(
-        (
-            jnp.moveaxis(item, 1, 0)
-            for item in (reception_vectors, address_vectors, payload_vectors, decay, unit, rate)
-        )
-    )
-
-    def step(current, pieces):
-        recept_now, keys_now, values_now, decay_now, unit_now, rate_now = pieces
-        recall = jnp.einsum("bhij,bhj->bhi", current, unit_now, precision=lax.Precision.HIGHEST)
-        current = (
-            current * decay_now[:, :, None, :]
-            - recall[:, :, :, None] * (unit_now * rate_now)[:, :, None, :]
-            + values_now[:, :, :, None] * keys_now[:, :, None, :]
-        )
-        output = jnp.einsum("bhij,bhj->bhi", current, recept_now, precision=lax.Precision.HIGHEST)
-        return (current, output)
-
-    final, outputs = lax.scan(step, start, inputs)
-    return (final, jnp.moveaxis(outputs, 0, 1))
+def halves(x):
+    high = x.astype(jnp.bfloat16)
+    return high, (x - high.astype(jnp.float32)).astype(jnp.bfloat16)
+
+
+def rows_dot(a, b):
+    rows = a.shape[1]
+    a_high, a_low = halves(a)
+    b_high, b_low = halves(b)
+    dims = (((2,), (2,)), ((0,), (0,)))
+    both = lax.dot_general(
+        jnp.concatenate([a_high, a_low], 1), b_high, dims, preferred_element_type=jnp.float32
+    )
+    rest = lax.dot_general(a_high, b_low, dims, preferred_element_type=jnp.float32)
+    return both[:, :rows] + both[:, rows:] + rest
+
+
+def outer_dot(a, b):
+    a_high, a_low = halves(a)
+    b_high, b_low = halves(b)
+    return lax.dot_general(
+        jnp.concatenate([a_high, a_high, a_low], 1),
+        jnp.concatenate([b_high, b_low, b_high], 1),
+        (((1,), (1,)), ((0,), (0,))),
+        preferred_element_type=jnp.float32,
+    )
+
+
+def summed_speeds(speeds):
+    place = lax.broadcasted_iota(jnp.int32, speeds.shape, 1)
+    for shift in (1, 2, 4):
+        speeds = speeds + jnp.where(place >= shift, pltpu.roll(speeds, shift, 1), 0.0)
+    return speeds
+
+
+def mix_kernel(
+    x_ref, wr_ref, wk_ref, wv_ref, wg_ref, speed_ref, rate_ref, boost_ref, scale_ref, state_ref,
+    new_ref, gated_ref, acc,
+):
+    step = pl.program_id(0)
+
+    @pl.when(step == 0)
+    def _():
+        acc[...] = jnp.zeros_like(acc)
+
+    x = x_ref[...]
+    for n, w_ref in enumerate((wr_ref, wk_ref, wv_ref, wg_ref)):
+        acc[n] += jnp.dot(x, w_ref[...], preferred_element_type=jnp.float32)
+
+    @pl.when(step == pl.num_programs(0) - 1)
+    def _():
+        seqs, lanes, size, _ = state_ref.shape
+        shape = (seqs, -1, size)
+        line = lax.broadcasted_iota(jnp.int32, (1, 16, 16), 1)
+        source = lax.broadcasted_iota(jnp.int32, (1, 16, 16), 2) % 8
+        seen = source < jnp.where(line < 8, line, line - 7)
+        for h in range(lanes):
+            cut = slice(h * size, (h + 1) * size)
+            recept, keys, values, gate = (acc[n, :, cut].reshape(shape) for n in range(4))
+            speed = speed_ref[:, cut].reshape(shape)
+            spent = summed_speeds(speed)
+            last = spent[:, 7:8, :]
+            unit = keys * lax.rsqrt(jnp.mean(keys * keys, -1, keepdims=True) + 1e-06) / math.sqrt(size)
+            eased = unit * rate_ref[:, cut].reshape(shape)
+            grown = jnp.exp(spent)
+            asks = jnp.concatenate([unit * jnp.exp(speed - spent), recept * jnp.exp(-spent)], 1)
+            gains = jnp.concatenate([keys * grown, eased * grown], 1)
+            weights = jnp.where(seen, rows_dot(asks, gains), 0.0)
+            start = state_ref[:, h]
+            found = rows_dot(asks, start)
+            for t in range(8):
+                found = found + weights[:, :, t : t + 1] * values[:, t : t + 1, :]
+            for t in range(8):
+                found = found - weights[:, :, 8 + t : 9 + t] * found[:, t : t + 1, :]
+            recall, wkv = found[:, :8], found[:, 8:]
+            left = jnp.exp(spent - last)
+            new_ref[:, h] = start * jnp.exp(-last) + outer_dot(
+                jnp.concatenate([values, -recall], 1),
+                jnp.concatenate([keys * left, eased * left], 1),
+            )
+            center = wkv - jnp.mean(wkv, -1, keepdims=True)
+            mixed = (
+                center
+                * lax.rsqrt(jnp.mean(center * center, -1, keepdims=True) + 1e-05)
+                * scale_ref[:, cut].reshape(1, 1, size)
+            )
+            own = jnp.sum(recept * keys * boost_ref[:, cut].reshape(1, 1, size), -1, keepdims=True)
+            mixed = mixed + own * values
+            gated = mixed * jax.nn.sigmoid(gate)
+            gated_ref[:, cut] = gated.reshape(-1, size).astype(gated_ref.dtype)
+
+
+def mixed_tokens(x, wr, wk, wv, wg, speed, rate, boost, scale, state):
+    tokens, width = x.shape
+    columns = wr.shape[1]
+    depth = 512
+    whole = lambda *shape: pl.BlockSpec(shape, lambda k: (0,) * len(shape))
+    piece = pl.BlockSpec((depth, columns), lambda k: (k, 0))
+    return pl.pallas_call(
+        mix_kernel,
+        grid=(width // depth,),
+        in_specs=[pl.BlockSpec((tokens, depth), lambda k: (0, k)), piece, piece, piece, piece]
+        + [whole(tokens, columns)] * 2
+        + [whole(1, columns)] * 2
+        + [whole(*state.shape)],
+        out_specs=[whole(*state.shape), whole(tokens, columns)],
+        out_shape=[
+            jax.ShapeDtypeStruct(state.shape, jnp.float32),
+            jax.ShapeDtypeStruct((tokens, columns), jnp.bfloat16),
+        ],
+        scratch_shapes=[pltpu.VMEM((4, tokens, columns), jnp.float32)],
+        compiler_params=pltpu.CompilerParams(vmem_limit_bytes=40 * 1024 * 1024),
+        name="mix",
+    )(x, wr, wk, wv, wg, speed, rate, boost.reshape(1, -1), scale.reshape(1, -1), state)
 
 
 def combine_stats(first, second):
@@ -153,51 +243,20 @@
     threshold_milli_nats,
 ):
     seq_dev, draft_len = proposed_tokens_list.shape
-    lanes_on_shard, subspace_size = (
-        recurrent_memory_matrix.shape[1],
-        recurrent_memory_matrix.shape[2],
-    )
     tok_dev = seq_dev * draft_len
     width = incoming_hidden_stream.shape[1]
-    shape4 = (seq_dev, draft_len, lanes_on_shard, subspace_size)
-    reception_vectors = jnp.dot(
-        incoming_hidden_stream, reception_projection, preferred_element_type=jnp.float32
-    ).reshape(shape4)
-    address_vectors = jnp.dot(
-        incoming_hidden_stream, address_projection, preferred_element_type=jnp.float32
-    ).reshape(shape4)
-    payload_vectors = jnp.dot(
-        incoming_hidden_stream, payload_projection, preferred_element_type=jnp.float32
-    ).reshape(shape4)
-    gate = jnp.dot(
-        incoming_hidden_stream, sigmoid_filter_matrix, preferred_element_type=jnp.float32
-    )
-    decay = jnp.exp(-forgetting_speed).reshape(shape4)
-    rate = adaptation_step_size.reshape(shape4)
-    new_state, wkv = advance(
-        recurrent_memory_matrix, reception_vectors, address_vectors, payload_vectors, decay, rate
-    )
-    center = wkv - jnp.mean(wkv, -1, keepdims=True)
-    interpolated_embedding = (
-        center
-        * lax.rsqrt(jnp.mean(center * center, -1, keepdims=True) + 1e-05)
-        * subspace_standardize_scale.reshape(lanes_on_shard, subspace_size)
-    )
-    interpolated_embedding = (
-        interpolated_embedding
-        + jnp.sum(
-            reception_vectors
-            * address_vectors
-            * diagonal_boost.reshape(lanes_on_shard, subspace_size),
-            -1,
-            keepdims=True,
-        )
-        * payload_vectors
-    )
-    gated = (
-        interpolated_embedding.reshape(tok_dev, lanes_on_shard * subspace_size)
-        * jax.nn.sigmoid(gate)
-    ).astype(jnp.bfloat16)
+    new_state, gated = mixed_tokens(
+        incoming_hidden_stream,
+        reception_projection,
+        address_projection,
+        payload_projection,
+        sigmoid_filter_matrix,
+        forgetting_speed,
+        adaptation_step_size,
+        diagonal_boost,
+        subspace_standardize_scale,
+        recurrent_memory_matrix,
+    )
     partial_out = jnp.dot(gated, emission_projection, preferred_element_type=jnp.float32)
     share = sent_and_summed(partial_out, HEAD, 1)
     cols = share.shape[1]

time: 321 us -> 207 us (0.64)
  matrix products: 84.9 us -> 8.72 us
  other arithmetic: 29.1 us -> 4.61 us
  local copies, waits for them, and re-layouts: 41.7 us -> 18.8 us
  Pallas kernels: 0 us -> 11.8 us
    dot_general x19 -> x0, matrix products: 72.4 us -> none  [the longest x8 39.5 us: step(): jnp.einsum('bhij,bhj->bhi', current, unit_now, precision=lax.Precision.HI...]
    mul x18 -> x0, local copies, waits for them, and re-layouts: 14.4 us -> none  [the longest x8 7.48 us: step(): values_now[:, :, :, None] * keys_now[:, :, None, :]]
    add x9 -> x0, other arithmetic: 13.8 us -> none  [the longest x8 12.3 us: step(): current * decay_now[:, :, None, :]]
    pallas_call x0 -> x1, Pallas kernels: none -> 11.8 us  [mixed_tokens(): pl.pallas_call(mix_kernel, grid=(width // depth,), in_specs=[pl.BlockSpec...]
    unnamed x21 -> x30, local copies, waits for them, and re-layouts: 4.79 us -> 13.9 us
    dynamic_slice x8 -> x0, local copies, waits for them, and re-layouts: 6.3 us -> none  [advance(): final, outputs = lax.scan(step, start, inputs)]
    mul x8 -> x0, other arithmetic: 6.28 us -> none  [step(): unit_now * rate_now]
    reshape x6 -> x1, local copies, waits for them, and re-layouts: 5.37 us -> 0.01 us  [gathered_once(): share = both[:, at:at + len(line)].reshape(len(both), -1)]
where the time goes in v1:
time: 207 us
  waiting for transfers between devices  82.3 us (40%)
  blocking collectives  47 us (23%)
  starting transfers between devices  19.2 us (9%)
  local copies, waits for them, and re-layouts  18.8 us (9%)
  between operations  14.3 us (7%)
  Pallas kernels  11.8 us (6%)
  matrix products  8.72 us (4%)
  other arithmetic  4.61 us (2%)
    all_gather x1, waiting for transfers between devices, shards(): lax.all_gather(normed, 'batch', axis=0, tiled=True)  37.6 us
    all_to_all x1, waiting for transfers between devices, sent_and_summed(): parts = lax.all_to_all(in_blocks(x, dim, size), axis, 0, 0, tiled=True)  31 us
    psum x2, blocking collectives, by_axis(): x = lax.psum(x, axis)  17.2 us
    all_to_all x1, blocking collectives, sent_to_all(): return lax.all_to_all(copies, axis, split_axis=0, concat_axis=0, tiled=True)  16.6 us
    unnamed x30, local copies, waits for them, and re-layouts  13.9 us
    all_to_all x2, waiting for transfers between devices, sent_to_all(): return lax.all_to_all(copies, axis, split_axis=0, concat_axis=0, tiled=True)  13.6 us
    all_gather x1, blocking collectives, shards(): lax.all_gather(proposed_tokens_list, 'batch', axis=0, tiled=True)  13.2 us
    pallas_call x1, Pallas kernels, mixed_tokens(): pl.pallas_call(mix_kernel, grid=(width // depth,), in_specs=[pl.BlockSpec...  11.8 us
  transfers between devices with their start and end apart: 4, of which 4 were waited for; matrix products, arithmetic and copies ran while one was open for 0% of the time, Pallas kernels for 0%

profile of v1, /device:TPU:0, one launch (start us, length us, event | category | flops | bytes accessed | tf_op | source)
XLA Modules:
  0.0 206.7 jit_solution(6907781997370275649)
XLA Ops:
  7.2 0.0 copy-start
  7.2 1.7 copy-done.1
  8.9 1.6 copy-done.2
  10.5 1.6 copy-done.3
  12.1 1.6 copy-done.4
  13.7 1.6 copy-done.5
  15.3 1.2 copy-done.6
  16.5 0.9 copy-done.7
  17.4 0.9 copy-done.8
  18.3 0.7 copy-done.9
  19.0 0.7 copy-done.10
  19.7 11.8 %mix.1 = (f32[16,4,64,64]{3,2,1,0:T(8,128)}, bf16[128,256]{1,0:T(8,128)(2,1)S(1)}) custom-call(bf16[128,4096]{1,0:T(8,128)(2,1)S(1)} %copy-done.6, bf16[4096,256]{1,0:T(8,128)(2,1)S(1)} %copy-done.1, bf16[4096,256]{1,0:T(8,128)(2,1)S(1)} %copy-done.2, bf16[4096,256]{1,0:T(8,128)(2,1)S(1)} %copy-done.3, bf16[4096,256]{1,0:T(8,128)(2,1)S(1)} %copy-done.4, ...), custom_call_target="tpu_custom_call" | custom-call | tf_op jit(solution)/shard_map/mix/pallas_call | solution.py:196
  31.5 0.4 fusion.16
  31.9 1.5 copy.46
  33.5 8.2 %all-to-all-start = ((f32[16,128,256]{2,1,0:T(8,128)}), f32[16,128,256]{2,1,0:T(8,128)}, u32[]{:S(2)}, u32[]{:S(2)}) async-start(f32[16,128,256]{2,1,0:T(8,128)} %bitcast.36), calls=%async_computation | async-start | bytes 4194304 | tf_op jit(solution)/shard_map/all_to_all | solution.py:22
  41.7 0.0 all-gather.3.cloned.1.call-start
  41.7 0.8 dynamic_slice.16
  42.5 31.0 %all-to-all-done = f32[16,128,256]{2,1,0:T(8,128)} async-done(((f32[16,128,256]{2,1,0:T(8,128)}), f32[16,128,256]{2,1,0:T(8,128)}, u32[]{:S(2)}, u32[]{:S(2)}) %all-to-all-start) | async-done | bytes 2097184 | tf_op jit(solution)/shard_map/all_to_all | solution.py:22
  73.5 1.7 reduce_sum.45
  75.3 1.0 fusion
  76.2 9.5 %all-reduce.1 = (f32[128]{0:T(128)S(1)}, f32[128]{0:T(128)S(1)}) all-reduce(f32[128]{0:T(128)S(1)} %get-tuple-element.19, f32[128]{0:T(128)S(1)} %get-tuple-element.18), channel_id=1, replica_groups=mesh['head_0'=4,'head_1'=4,'batch'=8] {'head_0'}, use_global_device_ids=true, to_apply=%region_5.0 | all-reduce | flops 256 | bytes 2048 | tf_op jit(solution)/shard_map/psum | solution.py:28
  85.7 7.7 %all-reduce = (f32[128]{0:T(128)S(1)}, f32[128]{0:T(128)S(1)}) all-reduce(f32[128]{0:T(128)S(1)} %get-tuple-element.22, f32[128]{0:T(128)S(1)} %get-tuple-element.23), channel_id=1, replica_groups=mesh['head_0'=4,'head_1'=4,'batch'=8] {'head_1'}, use_global_device_ids=true, to_apply=%region_6.0 | all-reduce | flops 256 | bytes 2048 | tf_op jit(solution)/shard_map/psum | solution.py:28
  93.4 0.9 multiply_convert_fusion
  94.4 0.1 copy.27
  94.5 0.0 copy-start.11
  94.5 0.2 broadcast_in_dim.18
  94.7 16.6 %all_to_all.20 = bf16[16,128,256]{1,2,0:T(8,128)(2,1)} all-to-all(bf16[16,128,256]{1,2,0:T(8,128)(2,1)S(1)} %broadcast_in_dim.18), channel_id=1, replica_groups=mesh['head_0'=4,'head_1'=4,'batch'=8] {'head_0','head_1'}, dimensions={0} | all-to-all | bytes 2097152 | tf_op jit(solution)/shard_map/all_to_all | solution.py:40
  111.3 0.0 all-gather.3.cloned.1.call-update
  111.4 13.2 %all-gather = s32[8,16,8]{1,2,0:T(8,128)S(1)} all-gather(s32[1,16,8]{1,2,0:T(8,128)S(1)} %bitcast.50), channel_id=1, replica_groups=mesh['head_0'=4,'head_1'=4,'batch'=8] {'batch'}, dimensions={0}, use_global_device_ids=true | all-gather | bytes 4608 | tf_op jit(solution)/shard_map/all_gather | solution.py:280
  124.6 0.1 copy.28
  124.7 0.1 sub.91
  124.8 37.6 %all-gather.3.cloned.1.call-done = bf16[1024,4096]{0,1:T(8,128)(2,1)} async-done(((bf16[128,4096]{0,1:T(8,128)(2,1)}), bf16[1024,4096]{0,1:T(8,128)(2,1)}) %all-gather.3.cloned.1.call-update) | async-done | bytes 8388624 | tf_op jit(solution)/shard_map/all_gather | solution.py:279
  162.4 8.3 %fusion.15 = (f32[1024]{0:T(1024)S(1)}, f32[1024,512]{0,1:T(8,128)S(1)}) fusion(bf16[1024,4096]{0,1:T(8,128)(2,1)} %all-gather.3.cloned.1.call-done, bf16[4096,512]{1,0:T(8,128)(2,1)} %param.27), kind=kOutput, calls=%fused_computation.47 | convolution fusion | flops 4295490560 | bytes 14684160 | tf_op jit(solution)/shard_map/dot_general | solution.py:282
  170.7 0.0 copy-start.12
  170.7 0.6 exponential_reduce_fusion
  171.3 0.7 broadcast_in_dim.20
  171.9 4.0 %all-to-all-start.2 = ((f32[8,3,1024]{2,1,0:T(4,128)}), f32[8,3,1024]{2,1,0:T(4,128)S(1)}, u32[]{:S(2)}, u32[]{:S(2)}) async-start(f32[8,3,1024]{2,1,0:T(4,128)} %broadcast_in_dim.20), calls=%async_computation.2 | async-start | bytes 262144 | tf_op jit(solution)/shard_map/all_to_all | solution.py:40
  175.9 6.1 %all-to-all-done.2 = f32[8,3,1024]{2,1,0:T(4,128)S(1)} async-done(((f32[8,3,1024]{2,1,0:T(4,128)}), f32[8,3,1024]{2,1,0:T(4,128)S(1)}, u32[]{:S(2)}, u32[]{:S(2)}) %all-to-all-start.2) | async-done | bytes 98336 | tf_op jit(solution)/shard_map/all_to_all | solution.py:40
  182.0 0.1 fusion.11
  182.6 0.6 broadcast_in_dim.21
  183.2 6.9 %all-to-all-start.3 = ((f32[16,3,128]{2,1,0:T(4,128)}), f32[16,3,128]{2,1,0:T(4,128)S(1)}, u32[]{:S(2)}, u32[]{:S(2)}) async-start(f32[16,3,128]{2,1,0:T(4,128)} %broadcast_in_dim.21), calls=%async_computation.3 | async-start | bytes 65536 | tf_op jit(solution)/shard_map/all_to_all | solution.py:40
  190.2 0.0 copy-done.12
  190.2 0.1 copy.33
  190.3 7.5 %all-to-all-done.3 = f32[16,3,128]{2,1,0:T(4,128)S(1)} async-done(((f32[16,3,128]{2,1,0:T(4,128)}), f32[16,3,128]{2,1,0:T(4,128)S(1)}, u32[]{:S(2)}, u32[]{:S(2)}) %all-to-all-start.3) | async-done | bytes 24608 | tf_op jit(solution)/shard_map/all_to_all | solution.py:40
  198.2 0.1 sub.107
  198.4 0.7 copy.34
  199.0 0.2 reduce_window.9
  199.2 0.7 copy.35
  (66 shorter events, 1.0 us)
Async XLA Ops:
  7.2 24.3 %copy-start = (bf16[256,4096]{1,0:T(8,128)(2,1)S(1)}, bf16[256,4096]{1,0:T(8,128)(2,1)}, u32[]{:S(2)}) copy-start(bf16[256,4096]{1,0:T(8,128)(2,1)} %param.25) | copy-start | bytes 6291460
  7.2 1.7 copy-start.1
  8.9 1.6 copy-start.2
  10.5 1.6 copy-start.3
  12.1 1.6 copy-start.4
  13.7 1.6 copy-start.5
  15.3 1.2 copy-start.6
  16.5 0.9 copy-start.7
  17.4 0.9 copy-start.8
  18.3 0.7 copy-start.9
  19.0 0.7 copy-start.10
  33.5 40.1 %all-to-all-start = ((f32[16,128,256]{2,1,0:T(8,128)}), f32[16,128,256]{2,1,0:T(8,128)}, u32[]{:S(2)}, u32[]{:S(2)}) async-start(f32[16,128,256]{2,1,0:T(8,128)} %bitcast.36), calls=%async_computation | async-start | bytes 4194304 | tf_op jit(solution)/shard_map/all_to_all | solution.py:22
  41.7 120.7 %all-gather.3.cloned.1.call-start = ((), (), s32[]{:S(2)}) async-start(), calls=%async_computation.4 | async-start | bytes 9437184 | tf_op jit(solution)/shard_map/all_gather | solution.py:279
  94.5 16.9 %copy-start.11 = (s32[16,8]{0,1:T(8,128)S(1)}, s32[16,8]{0,1:T(8,128)}, u32[]{:S(2)}) copy-start(s32[16,8]{0,1:T(8,128)} %param.28) | copy-start | bytes 1540
  170.7 19.5 %copy-start.12 = (s32[16,8]{0,1:T(8,128)S(1)}, s32[16,8]{0,1:T(8,128)}, u32[]{:S(2)}) copy-start(s32[16,8]{0,1:T(8,128)} %param.29) | copy-start | bytes 1540
  171.9 10.1 %all-to-all-start.2 = ((f32[8,3,1024]{2,1,0:T(4,128)}), f32[8,3,1024]{2,1,0:T(4,128)S(1)}, u32[]{:S(2)}, u32[]{:S(2)}) async-start(f32[8,3,1024]{2,1,0:T(4,128)} %broadcast_in_dim.20), calls=%async_computation.2 | async-start | bytes 262144 | tf_op jit(solution)/shard_map/all_to_all | solution.py:40
  183.2 14.6 %all-to-all-start.3 = ((f32[16,3,128]{2,1,0:T(4,128)}), f32[16,3,128]{2,1,0:T(4,128)S(1)}, u32[]{:S(2)}, u32[]{:S(2)}) async-start(f32[16,3,128]{2,1,0:T(4,128)} %broadcast_in_dim.21), calls=%async_computation.3 | async-start | bytes 65536 | tf_op jit(solution)/shard_map/all_to_all | solution.py:40
Sparse Core Ops, SparseCore 0:
  111.5 50.8 all-gather.2
